TPU v7x, 32 devices: a whole 2x2x4 slice. The times are simulated.
32 devices in a mesh: gene: 8 (over z, x), cell: 4 (over y, core).
Axes of the slice: x: 2, y: 2, z: 4, core: 2. Of those that a mesh axis runs over, the one named last changes fastest.
Arguments:
- counts: bfloat16 [32768, 8192], P('gene', 'cell'), may hold values from -6 to 6
- loadings: float32 [32768, 128], P('gene'), may hold values from -0.03125 to 0.03125
- values: float32 [128], replicated, may hold values from 0.5 to 2
- test_matrix: bfloat16 [8192, 128], P('cell'), may hold values from -0.0625 to 0.0625
- tile_mask: int32 [128, 64], P('gene', 'cell'), may hold values 0 or 1
Outputs:
- new_loadings: float32 [32768, 128], P('gene')
- new_values: float32 [128], replicated
All inputs are finite; a program needn't handle non-finite values. No bound on the sum of `tile_mask` on one device may be relied on, other than what follows from the above.
Results may differ from a plain program's by a relative error of at most 0.0028.
Values sent between devices are 32-bit elements; how exact they have to be, the bound alone decides.
A program may use at most 128 MiB of HBM per device.

v0:
```python
import jax
import jax.numpy as jnp
from jax import lax
from jax.sharding import PartitionSpec as P

GENE_TILE = 256
CELL_TILE = 128
SWEEPS = 3


def contract(left, right):
    return lax.dot_general(
        left,
        right,
        (((0,), (0,)), ((), ())),
        precision=lax.Precision.HIGHEST,
        preferred_element_type=jnp.float32,
    )


def outer_rows(stacked):
    return lax.dot_general(
        stacked,
        stacked,
        (((1,), (1,)), ((), ())),
        precision=lax.Precision.HIGHEST,
        preferred_element_type=jnp.float32,
    )


def local(counts, loadings, values, test_matrix, tile_mask):
    highest = lax.Precision.HIGHEST
    gene_rows, cell_cols = counts.shape
    components = loadings.shape[1]
    sketch_width = test_matrix.shape[1]
    cells_total = cell_cols * lax.axis_size("cell")
    genes_total = gene_rows * lax.axis_size("gene")
    tile_wide = jnp.repeat(
        jnp.repeat(tile_mask.astype(jnp.bfloat16), GENE_TILE, axis=0), CELL_TILE, axis=1
    )
    masked = counts * tile_wide
    load_narrow = loadings.astype(jnp.bfloat16)
    proj_part = lax.dot_general(
        load_narrow, masked, (((0,), (0,)), ((), ())), preferred_element_type=jnp.float32
    )
    projection = lax.psum(proj_part, "gene")
    test_wide = test_matrix.astype(jnp.float32)
    raw_part = jnp.dot(masked, test_matrix, preferred_element_type=jnp.float32)
    small_part = jnp.dot(projection, test_wide, precision=highest)
    raw_sketch, small_sketch = lax.psum((raw_part, small_part), "cell")
    sketch = raw_sketch - jnp.dot(loadings, small_sketch, precision=highest)
    sketch_gram = lax.psum(contract(sketch, sketch), "gene")
    factor = jnp.linalg.cholesky(sketch_gram)
    basis_rows = jax.scipy.linalg.solve_triangular(factor, sketch.T, lower=True)
    along_loadings = jnp.dot(basis_rows, loadings, precision=highest)
    coef = lax.psum(
        jnp.dot(basis_rows, masked, precision=highest, preferred_element_type=jnp.float32)
        - jnp.dot(along_loadings, projection, precision=highest),
        "gene",
    )
    stacked = jnp.concatenate([projection, coef], axis=0)
    core_sum = lax.psum(outer_rows(stacked), "cell")
    squares = jnp.concatenate([values * values, jnp.zeros((sketch_width,), jnp.float32)])
    core_matrix = core_sum / cells_total + jnp.diag(squares)
    subspace = jnp.eye(components + sketch_width, components, dtype=jnp.float32)
    for sweep in range(SWEEPS):
        image_block = jnp.dot(core_matrix, subspace, precision=highest)
        chol = jnp.linalg.cholesky(contract(image_block, image_block))
        subspace = jax.scipy.linalg.solve_triangular(chol, image_block.T, lower=True).T
    final_image = jnp.dot(core_matrix, subspace, precision=highest)
    new_values = jnp.sqrt(jnp.sum(subspace * final_image, axis=0))
    rotated = jnp.dot(loadings, subspace[:components], precision=highest) + contract(
        basis_rows, subspace[components:]
    )
    new_loadings = rotated * genes_total**0.5
    return (new_loadings, new_values)


def solution(mesh):
    placed = (P("gene", "cell"), P("gene", None), P(), P("cell", None), P("gene", "cell"))
    return jax.shard_map(
        local, mesh=mesh, in_specs=placed, out_specs=(P("gene", None), P()), check_vma=False
    )
```

profile of v0, /device:TPU:0, one launch (start us, length us, event | category | flops | bytes accessed | tf_op | source)
XLA Modules:
  0.0 522.0 jit_solution(2787085083832913234)
XLA Ops:
  7.2 0.7 convert_element_type.8
  8.1 19.0 %broadcast_in_dim.27 = bf16[4096,16,128]{2,1,0:T(8,128)(2,1)} broadcast(bf16[4096,16]{1,0:T(8,128)(2,1)S(1)} %bitcast.89), dimensions={0,1} | broadcast | bytes 16908288 | tf_op jit(solution)/shard_map/broadcast_in_dim | solution.py:38
  27.1 14.2 %convolution_bitcast_fusion.2 = f32[128,2048]{0,1:T(8,128)} fusion(f32[4096,128]{1,0:T(8,128)S(1)} %copy-done.1, bf16[4096,2048]{1,0:T(8,128)(2,1)} %param.8, bf16[512,8,16,128]{3,2,1,0:T(8,128)(2,1)} %bitcast.86), kind=kOutput, calls=%fused_computation.7 | convolution fusion | flops 2156396544 | bytes 36700160 | tf_op jit(solution)/shard_map/dot_general | solution.py:43
  41.3 15.6 %fusion.40 = f32[4096,128]{1,0:T(8,128)} fusion(bf16[2048,128]{1,0:T(8,128)(2,1)S(1)} %copy-done, bf16[4096,2048]{1,0:T(8,128)(2,1)} %param.8, bf16[512,8,16,128]{3,2,1,0:T(8,128)(2,1)} %bitcast.87), kind=kOutput, calls=%fused_computation.65 | convolution fusion | flops 2155872256 | bytes 36175872 | tf_op jit(solution)/shard_map/dot_general | solution.py:48
  56.9 65.6 %all-reduce.8.cloned.1.call-done = f32[128,2048]{0,1:T(8,128)} async-done(((f32[128,2048]{0,1:T(8,128)}), f32[128,2048]{0,1:T(8,128)}) %all-reduce.8.cloned.1.call-update) | async-done | bytes 1048592 | tf_op jit(solution)/shard_map/psum | solution.py:46
  122.5 2.8 fusion.41
  125.4 0.6 all-reduce.10.cloned.1.call-start
  126.0 51.7 %all-reduce.16.cloned.1.call-done = (f32[4096,128]{1,0:T(8,128)}, f32[128,128]{1,0:T(8,128)}) async-done(((f32[4096,128]{1,0:T(8,128)}, f32[128,128]{1,0:T(8,128)}), (f32[4096,128]{1,0:T(8,128)}, f32[128,128]{1,0:T(8,128)})) %all-reduce.16.cloned.1.call-update) | async-done | bytes 2162704 | tf_op jit(solution)/shard_map/psum | solution.py:50
  177.7 4.0 fusion.1
  181.7 4.1 fusion.42
  186.0 69.3 %all-reduce.10.cloned.1.call-done = f32[128,128]{0,1:T(8,128)} async-done(((f32[128,128]{0,1:T(8,128)}), f32[128,128]{0,1:T(8,128)}) %all-reduce.10.cloned.1.call-update) | async-done | bytes 65552 | tf_op jit(solution)/shard_map/psum | solution.py:52
  255.3 0.9 copy.9
  256.3 0.9 fusion.29
  257.1 11.7 %cholesky.74 = f32[128,128]{1,0:T(8,128)S(1)} custom-call(f32[128,128]{1,0:T(8,128)S(1)} %fusion.29), custom_call_target="Cholesky" | custom-call | tf_op jit(solution)/shard_map/jit(cholesky)/cholesky | solution.py:53
  268.9 0.6 compare_reduce_fusion.3
  269.5 0.7 fusion.15
  270.2 9.8 %custom-call.9 = f32[1,128,128]{1,2,0:T(8,128)S(1)} custom-call(f32[1,128,128]{2,1,0:T(8,128)S(1)} %fusion.15), custom_call_target="InvertDiagBlocksLowerTriangular" | custom-call | tf_op jit(solution)/shard_map/jit(_solve_triangular)/triangular_solve | solution.py:54
  280.0 3.3 fusion.27
  283.2 27.7 %fusion.39 = f32[128,2048]{0,1:T(8,128)} fusion(f32[128,4096]{1,0:T(8,128)} %fusion.27, bf16[4096,2048]{1,0:T(8,128)(2,1)} %param.8, bf16[512,8,16,128]{3,2,1,0:T(8,128)(2,1)} %bitcast.88), kind=kOutput, calls=%fused_computation.64 | convolution fusion | flops 12893290496 | bytes 36700160 | tf_op jit(solution)/shard_map/dot_general | solution.py:57
  310.9 3.9 fusion.43
  314.9 2.0 convolution_subtract_fusion
  316.9 0.5 all-reduce.14.cloned.1.call-start
  317.4 77.8 %all-reduce.12.cloned.1.call-done = f32[128,2048]{0,1:T(8,128)} async-done(((f32[128,2048]{0,1:T(8,128)}), f32[128,2048]{0,1:T(8,128)}) %all-reduce.12.cloned.1.call-update) | async-done | bytes 1048592 | tf_op jit(solution)/shard_map/psum | solution.py:56
  395.2 6.4 %fusion.2 = f32[256,256]{1,0:T(8,128)} fusion(f32[128,2048]{0,1:T(8,128)} %all-reduce.12.cloned.1.call-done, f32[128,2048]{0,1:T(8,128)} %all-reduce.8.cloned.1.call-done), kind=kOutput, calls=%fused_computation.8 | convolution fusion | flops 1611137024 | bytes 2359296 | tf_op jit(solution)/shard_map/dot_general | solution.py:22
  401.6 32.0 %all-reduce.14.cloned.1.call-done = f32[256,256]{1,0:T(8,128)} async-done(((f32[256,256]{1,0:T(8,128)}), f32[256,256]{1,0:T(8,128)}) %all-reduce.14.cloned.1.call-update) | async-done | bytes 262160 | tf_op jit(solution)/shard_map/psum | solution.py:62
  433.6 1.3 fusion.14
  435.0 0.4 fusion.44
  435.5 11.7 %cholesky.85 = f32[128,128]{1,0:T(8,128)S(1)} custom-call(f32[128,128]{1,0:T(8,128)S(1)} %fusion.26), custom_call_target="Cholesky" | custom-call | tf_op jit(solution)/shard_map/jit(cholesky)/cholesky | solution.py:68
  447.2 0.6 compare_reduce_fusion.2
  447.9 0.7 fusion.16
  448.5 9.8 %custom-call.12 = f32[1,128,128]{1,2,0:T(8,128)S(1)} custom-call(f32[1,128,128]{2,1,0:T(8,128)S(1)} %fusion.16), custom_call_target="InvertDiagBlocksLowerTriangular" | custom-call | tf_op jit(solution)/shard_map/jit(_solve_triangular)/triangular_solve | solution.py:69
  458.7 1.4 fusion.38
  460.0 0.4 fusion.45
  460.5 11.9 %cholesky.96 = f32[128,128]{1,0:T(8,128)S(1)} custom-call(f32[128,128]{1,0:T(8,128)S(1)} %fusion.24), custom_call_target="Cholesky" | custom-call | tf_op jit(solution)/shard_map/jit(cholesky)/cholesky | solution.py:68
  472.5 0.6 compare_reduce_fusion.1
  473.1 0.7 fusion.17
  473.8 9.8 %custom-call.13 = f32[1,128,128]{1,2,0:T(8,128)S(1)} custom-call(f32[1,128,128]{2,1,0:T(8,128)S(1)} %fusion.17), custom_call_target="InvertDiagBlocksLowerTriangular" | custom-call | tf_op jit(solution)/shard_map/jit(_solve_triangular)/triangular_solve | solution.py:69
  483.9 0.4 fusion.37
  484.3 0.4 fusion.46
  484.8 11.7 %cholesky.107 = f32[128,128]{1,0:T(8,128)S(1)} custom-call(f32[128,128]{1,0:T(8,128)S(1)} %fusion.22), custom_call_target="Cholesky" | custom-call | tf_op jit(solution)/shard_map/jit(cholesky)/cholesky | solution.py:68
  496.6 0.6 compare_reduce_fusion
  497.2 0.7 fusion.18
  497.9 10.0 %custom-call.14 = f32[1,128,128]{1,2,0:T(8,128)S(1)} custom-call(f32[1,128,128]{2,1,0:T(8,128)S(1)} %fusion.18), custom_call_target="InvertDiagBlocksLowerTriangular" | custom-call | tf_op jit(solution)/shard_map/jit(_solve_triangular)/triangular_solve | solution.py:69
  508.2 0.6 fusion.6
  508.8 0.5 sqrt.3
  509.3 2.0 convolution_bitcast_fusion
  511.3 2.1 fusion
  513.4 1.8 copy.15
  (40 shorter events, 1.9 us)
Async XLA Ops:
  7.2 34.2 %copy-start = (bf16[2048,128]{1,0:T(8,128)(2,1)S(1)}, bf16[2048,128]{1,0:T(8,128)(2,1)}, u32[]{:S(2)}) copy-start(bf16[2048,128]{1,0:T(8,128)(2,1)} %param.11) | copy-start | bytes 1572868
  7.2 115.3 %all-reduce.8.cloned.1.call-start = ((), (), s32[]{:S(2)}) async-start(), calls=%async_computation | async-start | bytes 2097152 | tf_op jit(solution)/shard_map/psum | solution.py:46
  8.1 19.0 %copy-start.1 = (f32[4096,128]{1,0:T(8,128)S(1)}, f32[4096,128]{1,0:T(8,128)}, u32[]{:S(2)}) copy-start(f32[4096,128]{1,0:T(8,128)} %param.9) | copy-start | bytes 6291460
  41.3 136.4 %all-reduce.16.cloned.1.call-start = ((), (), s32[]{:S(2)}) async-start(), calls=%async_computation.4 | async-start | bytes 4325376 | tf_op jit(solution)/shard_map/psum | solution.py:50
  125.4 129.9 %all-reduce.10.cloned.1.call-start = ((), (), s32[]{:S(2)}) async-start(), calls=%async_computation.1 | async-start | bytes 131072 | tf_op jit(solution)/shard_map/psum | solution.py:52
  185.8 209.4 %all-reduce.12.cloned.1.call-start = ((), (), s32[]{:S(2)}) async-start(), calls=%async_computation.2 | async-start | bytes 2097152 | tf_op jit(solution)/shard_map/psum | solution.py:56
  283.2 27.7 %copy-start.2 = (f32[4096,128]{1,0:T(8,128)S(1)}, f32[4096,128]{1,0:T(8,128)}, u32[]{:S(2)}) copy-start(f32[4096,128]{1,0:T(8,128)} %param.9) | copy-start | bytes 6291460
  310.9 3.9 copy-start.4
  310.9 3.9 copy-start.6
  316.9 84.7 %copy-start.7 = (f32[128]{0:T(128)S(1)}, f32[128]{0:T(128)}, u32[]{:S(2)}) copy-start(f32[128]{0:T(128)} %param.10) | copy-start | bytes 1540
  316.9 116.7 %all-reduce.14.cloned.1.call-start = ((), (), s32[]{:S(2)}) async-start(), calls=%async_computation.3 | async-start | bytes 524288 | tf_op jit(solution)/shard_map/psum | solution.py:62
  433.6 50.3 %copy-start.5 = (f32[256,256]{1,0:T(8,128)S(1)}, f32[256,256]{1,0:T(8,128)}, u32[]{:S(2)}) copy-start(f32[256,256]{1,0:T(8,128)} %all-reduce.14.cloned.1.call-done) | copy-start | bytes 786436
  509.3 2.0 copy-start.3
Sparse Core Ops, SparseCore 0:
  41.4 81.0 all-reduce.7
  125.6 52.0 all-reduce.15
  185.9 69.3 all-reduce.9
  317.0 78.1 all-reduce.11
  401.7 31.8 all-reduce.13
where the time goes:
time: 529 us; the launch traced here: 522 us
  waiting for transfers between devices  296 us (56%)
  matrix products  93.8 us (18%)
  other arithmetic  93.4 us (18%)
  local copies, waits for them, and re-layouts  22.7 us (4%)
  between operations  14.3 us (3%)
    psum x1, waiting for transfers between devices, local(): lax.psum(jnp.dot(basis_rows, masked, precision=highest, preferred_element...  77.8 us
    psum x1, waiting for transfers between devices, local(): sketch_gram = lax.psum(contract(sketch, sketch), 'gene')  69.3 us
    psum x1, waiting for transfers between devices, local(): projection = lax.psum(proj_part, 'gene')  65.6 us
    psum x1, waiting for transfers between devices, local(): raw_sketch, small_sketch = lax.psum((raw_part, small_part), 'cell')  51.7 us
    another operation x9, other arithmetic, local(): chol = jnp.linalg.cholesky(contract(image_block, image_block))  37.3 us
    psum x1, waiting for transfers between devices, local(): core_sum = lax.psum(outer_rows(stacked), 'cell')  32 us
    another operation x6, other arithmetic, local(): jax.scipy.linalg.solve_triangular(chol, image_block.T, lower=True)  31.6 us
    dot_general x1, matrix products, local(): jnp.dot(basis_rows, masked, precision=highest, preferred_element_type=jnp...  27.7 us
  transfers between devices with their start and end apart: 5, of which 5 were waited for; matrix products, arithmetic and copies ran while one was open for 3% of the time, Pallas kernels for 0%

commit v1 on v0

--- a/solution.py
+++ b/solution.py
@@ -49,7 +49,7 @@
     small_part = jnp.dot(projection, test_wide, precision=highest)
     raw_sketch, small_sketch = lax.psum((raw_part, small_part), "cell")
     sketch = raw_sketch - jnp.dot(loadings, small_sketch, precision=highest)
-    sketch_gram = lax.psum(contract(sketch, sketch), "gene")
+    sketch_gram = jnp.sum(lax.all_gather(contract(sketch, sketch), "gene"), axis=0)
     factor = jnp.linalg.cholesky(sketch_gram)
     basis_rows = jax.scipy.linalg.solve_triangular(factor, sketch.T, lower=True)
     along_loadings = jnp.dot(basis_rows, loadings, precision=highest)

time: 529 us -> 489 us (0.924)
  waiting for transfers between devices: 296 us -> 227 us
  blocking collectives: 0 us -> 31.7 us
    psum x1 -> x0, waiting for transfers between devices: 69.3 us -> none  [local(): sketch_gram = lax.psum(contract(sketch, sketch), 'gene')]
    all_gather x0 -> x1, blocking collectives: none -> 31.7 us  [local(): lax.all_gather(contract(sketch, sketch), 'gene')]
  transfers between devices with their start and end apart: 5 -> 4, of which waited for: 5 -> 4; matrix products, arithmetic and copies ran while one was open for 3% -> 3% of each run, Pallas kernels for 0% -> 0%
where the time goes in v1:
time: 489 us; the launch traced here: 482 us
  waiting for transfers between devices  227 us (46%)
  matrix products  93.1 us (19%)
  other arithmetic  92.6 us (19%)
  blocking collectives  31.7 us (6%)
  local copies, waits for them, and re-layouts  21.8 us (4%)
  between operations  14.3 us (3%)
    psum x1, waiting for transfers between devices, local(): lax.psum(jnp.dot(basis_rows, masked, precision=highest, preferred_element...  77.8 us
    psum x1, waiting for transfers between devices, local(): projection = lax.psum(proj_part, 'gene')  65.5 us
    psum x1, waiting for transfers between devices, local(): raw_sketch, small_sketch = lax.psum((raw_part, small_part), 'cell')  51.7 us
    another operation x9, other arithmetic, local(): chol = jnp.linalg.cholesky(contract(image_block, image_block))  37.3 us
    psum x1, waiting for transfers between devices, local(): core_sum = lax.psum(outer_rows(stacked), 'cell')  32 us
    all_gather x1, blocking collectives, local(): lax.all_gather(contract(sketch, sketch), 'gene')  31.7 us
    another operation x6, other arithmetic, local(): jax.scipy.linalg.solve_triangular(chol, image_block.T, lower=True)  31.6 us
    dot_general x1, matrix products, local(): jnp.dot(basis_rows, masked, precision=highest, preferred_element_type=jnp...  27.7 us
  transfers between devices with their start and end apart: 4, of which 4 were waited for; matrix products, arithmetic and copies ran while one was open for 3% of the time, Pallas kernels for 0%

profile of v1, /device:TPU:0, one launch (start us, length us, event | category | flops | bytes accessed | tf_op | source)
XLA Modules:
  0.0 481.8 jit_solution(9788520644005061528)
XLA Ops:
  7.2 0.7 convert_element_type.8
  8.1 19.0 %broadcast_in_dim.27 = bf16[4096,16,128]{2,1,0:T(8,128)(2,1)} broadcast(bf16[4096,16]{1,0:T(8,128)(2,1)S(1)} %bitcast.90), dimensions={0,1} | broadcast | bytes 16908288 | tf_op jit(solution)/shard_map/broadcast_in_dim | solution.py:38
  27.1 14.1 %convolution_bitcast_fusion.2 = f32[128,2048]{0,1:T(8,128)} fusion(f32[4096,128]{1,0:T(8,128)S(1)} %copy-done.1, bf16[4096,2048]{1,0:T(8,128)(2,1)} %param.8, bf16[512,8,16,128]{3,2,1,0:T(8,128)(2,1)} %bitcast.87), kind=kOutput, calls=%fused_computation.7 | convolution fusion | flops 2156396544 | bytes 36700160 | tf_op jit(solution)/shard_map/dot_general | solution.py:43
  41.3 15.6 %fusion.40 = f32[4096,128]{1,0:T(8,128)} fusion(bf16[2048,128]{1,0:T(8,128)(2,1)S(1)} %copy-done, bf16[4096,2048]{1,0:T(8,128)(2,1)} %param.8, bf16[512,8,16,128]{3,2,1,0:T(8,128)(2,1)} %bitcast.88), kind=kOutput, calls=%fused_computation.65 | convolution fusion | flops 2155872256 | bytes 36175872 | tf_op jit(solution)/shard_map/dot_general | solution.py:48
  56.9 65.5 %all-reduce.7.cloned.1.call-done = f32[128,2048]{0,1:T(8,128)} async-done(((f32[128,2048]{0,1:T(8,128)}), f32[128,2048]{0,1:T(8,128)}) %all-reduce.7.cloned.1.call-update) | async-done | bytes 1048592 | tf_op jit(solution)/shard_map/psum | solution.py:46
  122.4 2.8 fusion.41
  125.3 0.6 all-reduce.9.cloned.1.call-start
  125.8 51.7 %all-reduce.13.cloned.1.call-done = (f32[4096,128]{1,0:T(8,128)}, f32[128,128]{1,0:T(8,128)}) async-done(((f32[4096,128]{1,0:T(8,128)}, f32[128,128]{1,0:T(8,128)}), (f32[4096,128]{1,0:T(8,128)}, f32[128,128]{1,0:T(8,128)})) %all-reduce.13.cloned.1.call-update) | async-done | bytes 2162704 | tf_op jit(solution)/shard_map/psum | solution.py:50
  177.6 4.0 fusion.1
  181.6 3.5 fusion.42
  185.1 31.7 %all-gather = f32[1024,128]{1,0:T(8,128)S(1)} all-gather(f32[128,128]{1,0:T(8,128)S(1)} %fusion.42), channel_id=2, replica_groups=mesh['gene'=8,'cell'=4] {'gene'}, dimensions={0}, use_global_device_ids=true | all-gather | bytes 589824 | tf_op jit(solution)/shard_map/all_gather | solution.py:52
  217.0 11.7 %cholesky.74 = f32[128,128]{1,0:T(8,128)S(1)} custom-call(f32[128,128]{1,0:T(8,128)S(1)} %fusion.29), custom_call_target="Cholesky" | custom-call | tf_op jit(solution)/shard_map/jit(cholesky)/cholesky | solution.py:53
  228.7 0.6 compare_reduce_fusion.3
  229.3 0.7 fusion.15
  230.0 9.8 %custom-call.9 = f32[1,128,128]{1,2,0:T(8,128)S(1)} custom-call(f32[1,128,128]{2,1,0:T(8,128)S(1)} %fusion.15), custom_call_target="InvertDiagBlocksLowerTriangular" | custom-call | tf_op jit(solution)/shard_map/jit(_solve_triangular)/triangular_solve | solution.py:54
  239.8 3.3 fusion.27
  243.1 27.7 %fusion.39 = f32[128,2048]{0,1:T(8,128)} fusion(f32[128,4096]{1,0:T(8,128)} %fusion.27, bf16[4096,2048]{1,0:T(8,128)(2,1)} %param.8, bf16[512,8,16,128]{3,2,1,0:T(8,128)(2,1)} %bitcast.89), kind=kOutput, calls=%fused_computation.64 | convolution fusion | flops 12893290496 | bytes 36700160 | tf_op jit(solution)/shard_map/dot_general | solution.py:57
  270.8 3.9 fusion.43
  274.7 2.0 convolution_subtract_fusion
  276.7 0.5 all-reduce.11.cloned.1.call-start
  277.3 77.8 %all-reduce.9.cloned.1.call-done = f32[128,2048]{0,1:T(8,128)} async-done(((f32[128,2048]{0,1:T(8,128)}), f32[128,2048]{0,1:T(8,128)}) %all-reduce.9.cloned.1.call-update) | async-done | bytes 1048592 | tf_op jit(solution)/shard_map/psum | solution.py:56
  355.0 6.4 %fusion.2 = f32[256,256]{1,0:T(8,128)} fusion(f32[128,2048]{0,1:T(8,128)} %all-reduce.9.cloned.1.call-done, f32[128,2048]{0,1:T(8,128)} %all-reduce.7.cloned.1.call-done), kind=kOutput, calls=%fused_computation.8 | convolution fusion | flops 1611137024 | bytes 2359296 | tf_op jit(solution)/shard_map/dot_general | solution.py:22
  361.5 32.0 %all-reduce.11.cloned.1.call-done = f32[256,256]{1,0:T(8,128)} async-done(((f32[256,256]{1,0:T(8,128)}), f32[256,256]{1,0:T(8,128)}) %all-reduce.11.cloned.1.call-update) | async-done | bytes 262160 | tf_op jit(solution)/shard_map/psum | solution.py:62
  393.5 1.3 fusion.14
  394.8 0.4 fusion.44
  395.3 11.7 %cholesky.85 = f32[128,128]{1,0:T(8,128)S(1)} custom-call(f32[128,128]{1,0:T(8,128)S(1)} %fusion.26), custom_call_target="Cholesky" | custom-call | tf_op jit(solution)/shard_map/jit(cholesky)/cholesky | solution.py:68
  407.1 0.6 compare_reduce_fusion.2
  407.7 0.7 fusion.16
  408.4 9.8 %custom-call.12 = f32[1,128,128]{1,2,0:T(8,128)S(1)} custom-call(f32[1,128,128]{2,1,0:T(8,128)S(1)} %fusion.16), custom_call_target="InvertDiagBlocksLowerTriangular" | custom-call | tf_op jit(solution)/shard_map/jit(_solve_triangular)/triangular_solve | solution.py:69
  418.2 0.3 fusion.12
  418.5 1.4 fusion.38
  419.9 0.4 fusion.45
  420.4 11.9 %cholesky.96 = f32[128,128]{1,0:T(8,128)S(1)} custom-call(f32[128,128]{1,0:T(8,128)S(1)} %fusion.24), custom_call_target="Cholesky" | custom-call | tf_op jit(solution)/shard_map/jit(cholesky)/cholesky | solution.py:68
  432.3 0.6 compare_reduce_fusion.1
  432.9 0.7 fusion.17
  433.6 9.8 %custom-call.13 = f32[1,128,128]{1,2,0:T(8,128)S(1)} custom-call(f32[1,128,128]{2,1,0:T(8,128)S(1)} %fusion.17), custom_call_target="InvertDiagBlocksLowerTriangular" | custom-call | tf_op jit(solution)/shard_map/jit(_solve_triangular)/triangular_solve | solution.py:69
  443.4 0.3 fusion.10
  443.7 0.4 fusion.37
  444.2 0.4 fusion.46
  444.7 11.7 %cholesky.107 = f32[128,128]{1,0:T(8,128)S(1)} custom-call(f32[128,128]{1,0:T(8,128)S(1)} %fusion.22), custom_call_target="Cholesky" | custom-call | tf_op jit(solution)/shard_map/jit(cholesky)/cholesky | solution.py:68
  456.4 0.6 compare_reduce_fusion
  457.0 0.7 fusion.18
  457.7 10.0 %custom-call.14 = f32[1,128,128]{1,2,0:T(8,128)S(1)} custom-call(f32[1,128,128]{2,1,0:T(8,128)S(1)} %fusion.18), custom_call_target="InvertDiagBlocksLowerTriangular" | custom-call | tf_op jit(solution)/shard_map/jit(_solve_triangular)/triangular_solve | solution.py:69
  468.0 0.6 fusion.6
  468.6 0.5 sqrt.3
  469.1 2.0 convolution_bitcast_fusion
  471.1 2.1 fusion
  473.2 1.8 copy.22
  (39 shorter events, 1.2 us)
Async XLA Ops:
  7.2 34.1 %copy-start = (bf16[2048,128]{1,0:T(8,128)(2,1)S(1)}, bf16[2048,128]{1,0:T(8,128)(2,1)}, u32[]{:S(2)}) copy-start(bf16[2048,128]{1,0:T(8,128)(2,1)} %param.11) | copy-start | bytes 1572868
  7.2 115.2 %all-reduce.7.cloned.1.call-start = ((), (), s32[]{:S(2)}) async-start(), calls=%async_computation | async-start | bytes 2097152 | tf_op jit(solution)/shard_map/psum | solution.py:46
  8.1 19.0 %copy-start.1 = (f32[4096,128]{1,0:T(8,128)S(1)}, f32[4096,128]{1,0:T(8,128)}, u32[]{:S(2)}) copy-start(f32[4096,128]{1,0:T(8,128)} %param.9) | copy-start | bytes 6291460
  41.2 136.4 %all-reduce.13.cloned.1.call-start = ((), (), s32[]{:S(2)}) async-start(), calls=%async_computation.3 | async-start | bytes 4325376 | tf_op jit(solution)/shard_map/psum | solution.py:50
  125.3 229.8 %all-reduce.9.cloned.1.call-start = ((), (), s32[]{:S(2)}) async-start(), calls=%async_computation.1 | async-start | bytes 2097152 | tf_op jit(solution)/shard_map/psum | solution.py:56
  243.1 27.7 %copy-start.2 = (f32[4096,128]{1,0:T(8,128)S(1)}, f32[4096,128]{1,0:T(8,128)}, u32[]{:S(2)}) copy-start(f32[4096,128]{1,0:T(8,128)} %param.9) | copy-start | bytes 6291460
  270.8 3.9 copy-start.4
  270.8 3.9 copy-start.6
  276.7 84.7 %copy-start.7 = (f32[128]{0:T(128)S(1)}, f32[128]{0:T(128)}, u32[]{:S(2)}) copy-start(f32[128]{0:T(128)} %param.10) | copy-start | bytes 1540
  276.7 116.7 %all-reduce.11.cloned.1.call-start = ((), (), s32[]{:S(2)}) async-start(), calls=%async_computation.2 | async-start | bytes 524288 | tf_op jit(solution)/shard_map/psum | solution.py:62
  393.5 50.3 %copy-start.5 = (f32[256,256]{1,0:T(8,128)S(1)}, f32[256,256]{1,0:T(8,128)}, u32[]{:S(2)}) copy-start(f32[256,256]{1,0:T(8,128)} %all-reduce.11.cloned.1.call-done) | copy-start | bytes 786436
  469.1 2.0 copy-start.3
Sparse Core Ops, SparseCore 0:
  41.3 81.0 all-reduce.6
  125.5 52.0 all-reduce.12
  276.9 78.1 all-reduce.8
  361.5 31.8 all-reduce.10
